TPU v7x, 32 devices: a whole 2x2x4 slice. The times are simulated.
32 devices in a mesh: seq: 8 (over z, x), head: 4 (over y, core).
Axes of the slice: x: 2, y: 2, z: 4, core: 2. Of those that a mesh axis runs over, the one named last changes fastest.
Arguments:
- hidden_in: bfloat16 [4, 2048, 1024], P(None, ('seq', 'head')), may hold values from -6 to 6
- norm_gain1: float32 [1024], replicated, may hold values from 0.5 to 1.5
- w_query: bfloat16 [1024, 1024], P(None, 'head'), may hold values from -0.1875 to 0.1875
- w_key: bfloat16 [1024, 512], P(None, 'head'), may hold values from -0.1875 to 0.1875
- w_value: bfloat16 [1024, 512], P(None, 'head'), may hold values from -0.1875 to 0.1875
- w_out: bfloat16 [1024, 1024], P('head'), may hold values from -2 to 2
- norm_gain2: float32 [1024], replicated, may hold values from 0.5 to 1.5
- expert_gate: bfloat16 [16, 1024, 512], P('seq'), may hold values from -0.1875 to 0.1875
- expert_up: bfloat16 [16, 1024, 512], P('seq'), may hold values from -0.1875 to 0.1875
- expert_down: bfloat16 [16, 512, 1024], P('seq'), may hold values from -1 to 1
- routes: int32 [4, 2048, 8], P(None, ('seq', 'head')), may hold values from 0 to 15, all different within a row
- gate_weights: float32 [4, 2048, 8], P(None, ('seq', 'head')), may hold values from 0.05 to 0.25
- cotangent: bfloat16 [4, 2048, 1024], P(None, ('seq', 'head')), may hold values from -6 to 6
Outputs:
- layer_out: bfloat16 [4, 2048, 1024], P(None, ('seq', 'head'))
- input_grad: bfloat16 [4, 2048, 1024], P(None, ('seq', 'head'))
- norm_gain1_grad: float32 [1024], replicated
- w_query_grad: float32 [1024, 1024], P(None, 'head')
- w_key_grad: float32 [1024, 512], P(None, 'head')
- w_value_grad: float32 [1024, 512], P(None, 'head')
- w_out_grad: float32 [1024, 1024], P('head')
- norm_gain2_grad: float32 [1024], replicated
- expert_gate_grad: float32 [16, 1024, 512], P('seq')
- expert_up_grad: float32 [16, 1024, 512], P('seq')
- expert_down_grad: float32 [16, 512, 1024], P('seq')
Inputs may be any that keep to these rules, and one draw needn't show every extreme that they name: `routes`: each token names 8 different experts.
All inputs are finite; a program needn't handle non-finite values.
Results may differ from a plain program's by a relative error of at most 0.028.
Values may be sent and summed in bfloat16 or wider, within the bound.
No kernel may reach another device: no remote copies, remote signals or barrier semaphores. Data moves between devices by JAX's collectives and lax.ppermute only.
A program may use at most 192 MiB of HBM per device.

v0:
```python
import math

import jax
import jax.numpy as jnp
from jax import lax
from jax.sharding import PartitionSpec as P

HD = 64
TOP = 8


norm_eps = 1e-06
rope_base = 10000.0
masked_value = -1e30


def angle_tables(positions, head_dim):
    half_dim = head_dim // 2
    frequencies = jnp.exp(
        -jnp.log(rope_base) * jnp.arange(half_dim, dtype=jnp.float32) * 2.0 / head_dim
    )
    angles = positions.astype(jnp.float32)[:, None] * frequencies[None, :]
    return (jnp.cos(angles), jnp.sin(angles))


def rotate(values, cosine, sine_table):
    half_dim = values.shape[-1] // 2
    front_half = values[..., :half_dim]
    back_half = values[..., half_dim:]
    return jnp.concatenate(
        [
            front_half * cosine - back_half * sine_table,
            back_half * cosine + front_half * sine_table,
        ],
        -1,
    )


def rotate_back(values, cosine, sine_table):
    half_dim = values.shape[-1] // 2
    front_half = values[..., :half_dim]
    back_half = values[..., half_dim:]
    return jnp.concatenate(
        [
            front_half * cosine + back_half * sine_table,
            back_half * cosine - front_half * sine_table,
        ],
        -1,
    )


def norm_backward(values, inv_root, gain_vec, grad_normed):
    weighted = grad_normed * gain_vec
    gain_part = jnp.sum(grad_normed * values * inv_root, (0, 1))
    grad_values = inv_root * weighted - values * (inv_root * inv_root * inv_root) * jnp.mean(
        values * weighted, -1, keepdims=True
    )
    return (grad_values, gain_part)


def per_device(
    hidden_in,
    norm_gain1,
    w_query,
    w_key,
    w_value,
    w_out,
    norm_gain2,
    expert_gate,
    expert_up,
    expert_down,
    routes,
    gate_weights,
    cotangent,
):
    seqs_local, sub_rows, model_width = hidden_in.shape
    head_dim = HD
    kv_local = w_key.shape[1] // head_dim
    q_local = w_query.shape[1] // head_dim
    group_size = q_local // kv_local
    head_count = lax.axis_size("head")
    seq_count = lax.axis_size("seq")
    span_len = sub_rows * head_count
    total_len = span_len * seq_count
    experts_local = expert_gate.shape[0]
    expert_total = experts_local * seq_count
    capacity = seqs_local * sub_rows * TOP * 5 // (4 * expert_total)
    score_scale = 1.0 / math.sqrt(head_dim)
    seq_rank = lax.axis_index("seq")
    q_cols = q_local * head_dim
    k_cols = kv_local * head_dim
    x_float = hidden_in.astype(jnp.float32)
    inv_one = lax.rsqrt(jnp.mean(x_float * x_float, -1, keepdims=True) + norm_eps)
    normed_one = (x_float * inv_one * norm_gain1).astype(jnp.bfloat16)
    normed_all = lax.all_gather(normed_one, "head", axis=1, tiled=True)
    w_joint = jnp.concatenate([w_query, w_key, w_value], 1)
    joint_proj = jnp.dot(normed_all, w_joint, preferred_element_type=jnp.float32)
    positions = seq_rank * span_len + jnp.arange(span_len, dtype=jnp.int32)
    cosine, sine_table = angle_tables(positions, head_dim)
    cos_query = cosine[:, None, None, :]
    sin_query = sine_table[:, None, None, :]
    cos_key = cosine[:, None, :]
    sin_key = sine_table[:, None, :]
    query_lin = joint_proj[..., :q_cols].reshape(
        seqs_local, span_len, kv_local, group_size, head_dim
    )
    key_lin = joint_proj[..., q_cols : q_cols + k_cols].reshape(
        seqs_local, span_len, kv_local, head_dim
    )
    value_lin = joint_proj[..., q_cols + k_cols :].reshape(seqs_local, span_len, kv_local, head_dim)
    query_b = rotate(query_lin, cos_query, sin_query).astype(jnp.bfloat16)
    key_b = rotate(key_lin, cos_key, sin_key).astype(jnp.bfloat16)
    value_b = value_lin.astype(jnp.bfloat16)
    kv_own = jnp.concatenate([key_b, value_b], -1)
    kv_whole = lax.all_gather(kv_own, "seq", axis=1, tiled=True)
    block_len = min(512, span_len)
    block_count = (seq_rank + 1) * (span_len // block_len)
    key_offsets = jnp.arange(block_len, dtype=jnp.int32)

    def block_scores(block_idx):
        kv_block = lax.dynamic_slice_in_dim(kv_whole, block_idx * block_len, block_len, 1)
        key_block = kv_block[..., :head_dim]
        value_block = kv_block[..., head_dim:]
        scores = (
            jnp.einsum("scgrd,skgd->sgrck", query_b, key_block, preferred_element_type=jnp.float32)
            * score_scale
        )
        allowed = (block_idx * block_len + key_offsets)[None, :] <= positions[:, None]
        scores = jnp.where(allowed, scores, masked_value)
        return (scores, key_block, value_block)

    def forward_step(block_idx, running):
        run_max, run_sum, run_acc = running
        scores, key_block, value_block = block_scores(block_idx)
        new_max = jnp.maximum(run_max, jnp.max(scores, -1))
        factor = jnp.exp(run_max - new_max)
        block_probs = jnp.exp(scores - new_max[..., None])
        run_sum = run_sum * factor + jnp.sum(block_probs, -1)
        run_acc = run_acc * factor[..., None] + jnp.einsum(
            "sgrck,skgd->sgrcd",
            block_probs.astype(jnp.bfloat16),
            value_block,
            preferred_element_type=jnp.float32,
        )
        return (new_max, run_sum, run_acc)

    stat_shape = (seqs_local, kv_local, group_size, span_len)
    start_state = (
        jnp.full(stat_shape, masked_value, jnp.float32),
        jnp.zeros(stat_shape, jnp.float32),
        jnp.zeros(stat_shape + (head_dim,), jnp.float32),
    )
    run_max, run_sum, run_acc = lax.fori_loop(0, block_count, forward_step, start_state)
    log_sum = run_max + jnp.log(run_sum)
    attn_keep = (run_acc / run_sum[..., None]).transpose(0, 3, 1, 2, 4)
    attn_b = attn_keep.astype(jnp.bfloat16).reshape(seqs_local, span_len, q_cols)
    out_terms = jnp.dot(attn_b, w_out, preferred_element_type=jnp.float32)
    attn_out = lax.psum_scatter(
        out_terms.astype(jnp.bfloat16), "head", scatter_dimension=1, tiled=True
    ).astype(jnp.float32)
    resid = x_float + attn_out
    inv_two = lax.rsqrt(jnp.mean(resid * resid, -1, keepdims=True) + norm_eps)
    normed_two = (resid * inv_two * norm_gain2).astype(jnp.bfloat16)
    token_count = seqs_local * sub_rows
    pair_count = token_count * TOP
    route_flat = routes.reshape(pair_count)
    gate_flat = gate_weights.reshape(pair_count)
    onehot = (route_flat[:, None] == jnp.arange(expert_total, dtype=jnp.int32)[None, :]).astype(
        jnp.int32
    )
    pair_rank = jnp.sum((jnp.cumsum(onehot, 0) - onehot) * onehot, 1)
    pair_kept = pair_rank < capacity
    slot_target = jnp.where(pair_kept, route_flat * capacity + pair_rank, expert_total * capacity)
    slot_safe = jnp.where(pair_kept, route_flat * capacity + pair_rank, 0)
    slot_pair = (
        jnp.full((expert_total * capacity,), -1, jnp.int32)
        .at[slot_target]
        .set(jnp.arange(pair_count, dtype=jnp.int32), mode="drop")
    )
    slot_valid = slot_pair >= 0
    slot_token = jnp.where(slot_valid, slot_pair // TOP, 0)
    slot_gate = jnp.where(slot_valid, gate_flat[jnp.maximum(slot_pair, 0)], 0.0)
    normed_flat = normed_two.reshape(token_count, model_width)
    dispatch = jnp.where(slot_valid[:, None], normed_flat[slot_token], 0).reshape(
        expert_total, capacity, model_width
    )
    slot_rows = lax.all_to_all(dispatch, "seq", split_axis=0, concat_axis=0, tiled=True)
    grouped = slot_rows.reshape(-1, experts_local, slot_rows.shape[1], model_width)
    gate_lin = jnp.einsum(
        "sekd,edf->sekf", grouped, expert_gate, preferred_element_type=jnp.float32
    )
    up_lin = jnp.einsum("sekd,edf->sekf", grouped, expert_up, preferred_element_type=jnp.float32)
    hidden = (gate_lin * jax.nn.sigmoid(gate_lin) * up_lin).astype(jnp.bfloat16)
    outputs = jnp.einsum(
        "sekf,efd->sekd", hidden, expert_down, preferred_element_type=jnp.float32
    ).astype(jnp.bfloat16)
    expert_out = outputs.reshape(slot_rows.shape)
    returned = lax.all_to_all(expert_out, "seq", split_axis=0, concat_axis=0, tiled=True)
    returned_flat = returned.reshape(expert_total * capacity, model_width)
    pair_weight = jnp.where(pair_kept, gate_flat, 0.0)
    pair_rows = returned_flat[slot_safe].astype(jnp.float32) * pair_weight[:, None]
    mixture = jnp.sum(pair_rows.reshape(token_count, TOP, model_width), 1)
    final_sum = resid + mixture.reshape(seqs_local, sub_rows, model_width)
    layer_out = final_sum.astype(jnp.bfloat16)
    grad_out = cotangent.astype(jnp.float32)
    grad_flat = grad_out.reshape(token_count, model_width)
    slot_grads = (
        (slot_gate[:, None] * grad_flat[slot_token])
        .astype(jnp.bfloat16)
        .reshape(expert_total, capacity, model_width)
    )
    grad_recv, rows_again = (
        lax.all_to_all(slot_grads, "seq", split_axis=0, concat_axis=0, tiled=True),
        lax.all_to_all(dispatch, "seq", split_axis=0, concat_axis=0, tiled=True),
    )
    grouped = rows_again.reshape(seq_count, experts_local, capacity, model_width)
    grad_grouped = grad_recv.reshape(seq_count, experts_local, capacity, model_width)
    gate_lin = jnp.einsum(
        "sekd,edf->sekf", grouped, expert_gate, preferred_element_type=jnp.float32
    )
    up_lin = jnp.einsum("sekd,edf->sekf", grouped, expert_up, preferred_element_type=jnp.float32)
    gate_sigmoid = jax.nn.sigmoid(gate_lin)
    silu_value = gate_lin * gate_sigmoid
    hidden = (silu_value * up_lin).astype(jnp.bfloat16)
    grad_hidden = jnp.einsum(
        "sekd,efd->sekf", grad_grouped, expert_down, preferred_element_type=jnp.float32
    )
    grad_down_w = jnp.einsum(
        "sekf,sekd->efd", hidden, grad_grouped, preferred_element_type=jnp.float32
    )
    grad_up_b = (grad_hidden * silu_value).astype(jnp.bfloat16)
    grad_gate_b = (
        grad_hidden * up_lin * gate_sigmoid * (1.0 + gate_lin * (1.0 - gate_sigmoid))
    ).astype(jnp.bfloat16)
    grad_gate_w = jnp.einsum(
        "sekd,sekf->edf", grouped, grad_gate_b, preferred_element_type=jnp.float32
    )
    grad_up_w = jnp.einsum("sekd,sekf->edf", grouped, grad_up_b, preferred_element_type=jnp.float32)
    grad_slot_in = jnp.einsum(
        "sekf,edf->sekd", grad_gate_b, expert_gate, preferred_element_type=jnp.float32
    ) + jnp.einsum("sekf,edf->sekd", grad_up_b, expert_up, preferred_element_type=jnp.float32)
    grad_slot_in = grad_slot_in.astype(jnp.bfloat16).reshape(
        seq_count * experts_local, capacity, model_width
    )
    grad_back = lax.all_to_all(grad_slot_in, "seq", split_axis=0, concat_axis=0, tiled=True)
    grad_back_flat = grad_back.reshape(expert_total * capacity, model_width)
    pair_grads = jnp.where(pair_kept[:, None], grad_back_flat[slot_safe].astype(jnp.float32), 0.0)
    grad_normed_two = jnp.sum(pair_grads.reshape(token_count, TOP, model_width), 1).reshape(
        seqs_local, sub_rows, model_width
    )
    grad_norm_two, gain_two_part = norm_backward(resid, inv_two, norm_gain2, grad_normed_two)
    grad_resid = grad_out + grad_norm_two
    grad_resid_b = grad_resid.astype(jnp.bfloat16)
    grad_all = lax.all_gather(grad_resid_b, "head", axis=1, tiled=True)
    grad_out_w = jnp.einsum("scq,scd->qd", attn_b, grad_all, preferred_element_type=jnp.float32)
    grad_attn = jnp.einsum(
        "scd,qd->scq", grad_all, w_out, preferred_element_type=jnp.float32
    ).astype(jnp.bfloat16)
    grad_attn = grad_attn.reshape(seqs_local, span_len, kv_local, group_size, head_dim)
    row_delta = jnp.einsum("scgrd,scgrd->sgrc", grad_attn.astype(jnp.float32), attn_keep)

    def backward_step(block_idx, running):
        grad_query, grad_kv = running
        scores, key_block, value_block = block_scores(block_idx)
        block_probs = jnp.exp(scores - log_sum[..., None])
        grad_value = jnp.einsum(
            "sgrck,scgrd->skgd",
            block_probs.astype(jnp.bfloat16),
            grad_attn,
            preferred_element_type=jnp.float32,
        )
        grad_probs = jnp.einsum(
            "scgrd,skgd->sgrck", grad_attn, value_block, preferred_element_type=jnp.float32
        )
        grad_scores = (block_probs * (grad_probs - row_delta[..., None]) * score_scale).astype(
            jnp.bfloat16
        )
        grad_query = grad_query + jnp.einsum(
            "sgrck,skgd->scgrd", grad_scores, key_block, preferred_element_type=jnp.float32
        )
        grad_key = jnp.einsum(
            "sgrck,scgrd->skgd", grad_scores, query_b, preferred_element_type=jnp.float32
        )
        grad_kv = lax.dynamic_update_slice_in_dim(
            grad_kv, jnp.concatenate([grad_key, grad_value], -1), block_idx * block_len, 1
        )
        return (grad_query, grad_kv)

    back_state = (
        jnp.zeros(query_lin.shape, jnp.float32),
        jnp.zeros((seqs_local, total_len, kv_local, 2 * head_dim), jnp.float32),
    )
    grad_query, grad_kv = lax.fori_loop(0, block_count, backward_step, back_state)
    grad_kv_own = lax.psum_scatter(
        grad_kv.astype(jnp.bfloat16), "seq", scatter_dimension=1, tiled=True
    ).astype(jnp.float32)
    grad_query_b = (
        rotate_back(grad_query, cos_query, sin_query)
        .astype(jnp.bfloat16)
        .reshape(seqs_local, span_len, q_cols)
    )
    grad_key_b = (
        rotate_back(grad_kv_own[..., :head_dim], cos_key, sin_key)
        .astype(jnp.bfloat16)
        .reshape(seqs_local, span_len, k_cols)
    )
    grad_value_b = (
        grad_kv_own[..., head_dim:].astype(jnp.bfloat16).reshape(seqs_local, span_len, k_cols)
    )
    grad_joint = jnp.concatenate([grad_query_b, grad_key_b, grad_value_b], -1)
    grad_w_joint = jnp.einsum(
        "scd,sco->do", normed_all, grad_joint, preferred_element_type=jnp.float32
    )
    grad_normed_part = jnp.einsum(
        "sco,do->scd", grad_joint, w_joint, preferred_element_type=jnp.float32
    )
    grad_normed_one = lax.psum_scatter(
        grad_normed_part.astype(jnp.bfloat16), "head", scatter_dimension=1, tiled=True
    ).astype(jnp.float32)
    grad_norm_one, gain_one_part = norm_backward(x_float, inv_one, norm_gain1, grad_normed_one)
    input_grad = (grad_resid + grad_norm_one).astype(jnp.bfloat16)
    gate_total, up_total, down_total, gain_one_head, gain_two_head = (
        lax.psum(grad_gate_w.astype(jnp.bfloat16), "head").astype(jnp.float32),
        lax.psum(grad_up_w.astype(jnp.bfloat16), "head").astype(jnp.float32),
        lax.psum(grad_down_w.astype(jnp.bfloat16), "head").astype(jnp.float32),
        lax.psum(gain_one_part.astype(jnp.bfloat16), "head").astype(jnp.float32),
        lax.psum(gain_two_part.astype(jnp.bfloat16), "head").astype(jnp.float32),
    )
    query_total, key_total, value_total, out_total, gain_one_total, gain_two_total = (
        lax.psum(grad_w_joint[:, :q_cols].astype(jnp.bfloat16), "seq").astype(jnp.float32),
        lax.psum(grad_w_joint[:, q_cols : q_cols + k_cols].astype(jnp.bfloat16), "seq").astype(
            jnp.float32
        ),
        lax.psum(grad_w_joint[:, q_cols + k_cols :].astype(jnp.bfloat16), "seq").astype(
            jnp.float32
        ),
        lax.psum(grad_out_w.astype(jnp.bfloat16), "seq").astype(jnp.float32),
        lax.psum(gain_one_head.astype(jnp.bfloat16), "seq").astype(jnp.float32),
        lax.psum(gain_two_head.astype(jnp.bfloat16), "seq").astype(jnp.float32),
    )
    return (
        layer_out,
        input_grad,
        gain_one_total,
        query_total,
        key_total,
        value_total,
        out_total,
        gain_two_total,
        gate_total,
        up_total,
        down_total,
    )


def solution(mesh):
    return jax.shard_map(
        per_device,
        mesh=mesh,
        in_specs=(
            P(None, ("seq", "head"), None),
            P(),
            P(None, "head"),
            P(None, "head"),
            P(None, "head"),
            P("head", None),
            P(),
            P("seq", None, None),
            P("seq", None, None),
            P("seq", None, None),
            P(None, ("seq", "head"), None),
            P(None, ("seq", "head"), None),
            P(None, ("seq", "head"), None),
        ),
        out_specs=(
            P(None, ("seq", "head"), None),
            P(None, ("seq", "head"), None),
            P(),
            P(None, "head"),
            P(None, "head"),
            P(None, "head"),
            P("head", None),
            P(),
            P("seq", None, None),
            P("seq", None, None),
            P("seq", None, None),
        ),
        check_vma=False,
    )
```

profile of v0, /device:TPU:0, one launch (start us, length us, event | category | flops | bytes accessed | tf_op | source)
XLA Modules:
  0.0 1255.9 jit_solution(6174229261013702106)
XLA Ops:
  12.1 25.1 %all-gather.4.cloned.1.call-done = bf16[4,256,1024]{2,1,0:T(8,128)(2,1)} async-done(((bf16[4,64,1024]{2,1,0:T(8,128)(2,1)}), bf16[4,256,1024]{2,1,0:T(8,128)(2,1)}) %all-gather.4.cloned.1.call-update) | async-done | bytes 2097168 | tf_op jit(solution)/shard_map/all_gather | solution.py:95
  47.2 70.7 %all-gather.6.cloned.1.call-done = bf16[4,2048,2,128]{1,3,2,0:T(8,128)(2,1)} async-done(((bf16[4,256,2,128]{1,3,2,0:T(8,128)(2,1)}), bf16[4,2048,2,128]{1,3,2,0:T(8,128)(2,1)}) %all-gather.6.cloned.1.call-update) | async-done | bytes 4194320 | tf_op jit(solution)/shard_map/all_gather | solution.py:115
  118.9 9.5 while.28
  139.7 8.1 scatter_custom_fusion
  147.8 13.6 %gather_fusion.2 = f32[2560]{0:T(1024)S(1)} fusion(f32[2048]{0:T(1024)S(1)} %reshape.377, s32[3072]{0:T(1024)S(1)} %pad_clamp_fusion), kind=kCustom, calls=%fused_computation.2 | custom fusion | bytes 30720 | tf_op jit(solution)/shard_map/gather | solution.py:182
  161.6 67.3 %reduce-scatter.4.cloned.1.call-done = bf16[4,64,1024]{2,1,0:T(8,128)(2,1)} async-done(((bf16[4,256,1024]{2,1,0:T(8,128)(2,1)}), bf16[4,64,1024]{2,1,0:T(8,128)(2,1)}) %reduce-scatter.4.cloned.1.call-update) | async-done | bytes 524304 | tf_op jit(solution)/shard_map/reduce_scatter | solution.py:158
  232.0 8.8 gather_fusion
  252.7 9.0 gather_fusion.3
  268.7 98.4 %all-to-all-done = bf16[16,160,1024]{2,1,0:T(8,128)(2,1)} async-done(((bf16[16,160,1024]{2,1,0:T(8,128)(2,1)}), bf16[16,160,1024]{2,1,0:T(8,128)(2,1)}, u32[]{:S(2)}, u32[]{:S(2)}) %all-to-all-start) | async-done | bytes 5242912 | tf_op jit(solution)/shard_map/all_to_all | solution.py:187
  372.3 8.4 fusion.60
  387.9 99.3 %all-to-all-done.2 = bf16[16,160,1024]{2,1,0:T(8,128)(2,1)} async-done(((bf16[16,160,1024]{2,1,0:T(8,128)(2,1)}), bf16[16,160,1024]{2,1,0:T(8,128)(2,1)}, u32[]{:S(2)}, u32[]{:S(2)}) %all-to-all-start.2) | async-done | bytes 5242912 | tf_op jit(solution)/shard_map/all_to_all | solution.py:213
  487.2 11.2 fusion.50
  514.9 114.5 %all-to-all-done.3 = bf16[16,160,1024]{2,1,0:T(8,128)(2,1)} async-done(((bf16[16,160,1024]{2,1,0:T(8,128)(2,1)}), bf16[16,160,1024]{2,1,0:T(8,128)(2,1)}, u32[]{:S(2)}, u32[]{:S(2)}) %all-to-all-start.3) | async-done | bytes 5242912 | tf_op jit(solution)/shard_map/all_to_all | solution.py:245
  629.5 14.1 %gather_fusion.4 = bf16[2048,1024]{1,0:T(8,128)(2,1)} fusion(bf16[2560,1024]{1,0:T(8,128)(2,1)} %bitcast.39, s32[2048]{0:T(1024)S(1)} %broadcast_clamp_fusion), kind=kCustom, calls=%fused_computation.4 | custom fusion | bytes 8396800 | tf_op jit(solution)/shard_map/gather | solution.py:247
  650.4 20.7 %all-gather.8.cloned.1.call-done = bf16[4,256,1024]{2,1,0:T(8,128)(2,1)} async-done(((bf16[4,64,1024]{2,1,0:T(8,128)(2,1)}), bf16[4,256,1024]{2,1,0:T(8,128)(2,1)}) %all-gather.8.cloned.1.call-update) | async-done | bytes 2097168 | tf_op jit(solution)/shard_map/all_gather | solution.py:254
  678.4 13.3 %while.29 = (s32[]{:T(128)}, f32[4,256,2,2,64]{1,4,3,2,0:T(8,128)}, bf16[4,2048,2,128]{1,3,2,0:T(8,128)(2,1)}, s32[]{:T(128)}, bf16[4,2048,2,128]{1,3,2,0:T(8,12...) while((s32[]{:T(128)}, f32[4,256,2,2,64]{1,4,3,2,0:T(8,128)}, ...), condition=%wide.region_15.16_spmd.clone, body=%wide.region_14.15_spmd.clone.sunk | while | flops 683999744 | bytes 44552476 | solution.py:293
  699.8 98.7 %all-to-all-start.1 = ((bf16[16,160,1024]{2,1,0:T(8,128)(2,1)}), bf16[16,160,1024]{2,1,0:T(8,128)(2,1)}, u32[]{:S(2)}, u32[]{:S(2)}) async-start(bf16[16,160,1024]{2,1,0:T(8,128)(2,1)} %bitcast.284), calls=%async_computation.2 | async-start | bytes 10485760 | tf_op jit(solution)/shard_map/all_to_all | solution.py:198
  806.4 8.0 bitcast_convert_fusion.2
  829.3 136.7 %reduce-scatter.6.cloned.1.call-done = bf16[4,256,2,128]{1,3,2,0:T(8,128)(2,1)} async-done(((bf16[4,2048,2,128]{1,3,2,0:T(8,128)(2,1)}), bf16[4,256,2,128]{1,3,2,0:T(8,128)(2,1)}) %reduce-scatter.6.cloned.1.call-update) | async-done | bytes 524304 | tf_op jit(solution)/shard_map/reduce_scatter | solution.py:294
  978.1 110.2 %all-reduce.9.cloned.1.call-done = (bf16[2,1024,512]{2,1,0:T(8,128)(2,1)}, bf16[2,1024,512]{2,1,0:T(8,128)(2,1)}, bf16[2,512,1024]{2,1,0:T(8,128)(2,1)}) async-done(((bf16[2,1024,512]{2,1,0:T(8,128)(2,1)}, bf16[2,1024,512]{2,1,0:T(8,128)(2,1)}, bf16[2,512,1024]{2,1,0:T(8,128)(2,1)}), (bf16[2,1024,512]{2,1,0:T(8,128)(2,1)}, bf16[2,1024,512]{2,1,0:T(8,128)(2,1)}, ...) | async-done | bytes 6291472 | tf_op jit(solution)/shard_map/psum | solution.py:323
  1097.7 14.4 %gather_fusion.1 = bf16[2048,1024]{1,0:T(8,128)(2,1)} fusion(bf16[2560,1024]{1,0:T(8,128)(2,1)} %bitcast.25, s32[2048]{0:T(1024)S(1)} %broadcast_clamp_fusion), kind=kCustom, calls=%fused_computation.1 | custom fusion | bytes 8396800 | tf_op jit(solution)/shard_map/gather | solution.py:201
  1118.0 64.4 %all-reduce.7.cloned.1.call-done = (bf16[1024,256]{1,0:T(8,128)(2,1)}, bf16[1024,128]{1,0:T(8,128)(2,1)}, bf16[1024,128]{1,0:T(8,128)(2,1)}, bf16[256,1024]{1,0:T(8,128)(2,1)}) async-done(((bf16[1024,256]{1,0:T(8,128)(2,1)}, bf16[1024,128]{1,0:T(8,128)(2,1)}, bf16[1024,128]{1,0:T(8,128)(2,1)}, bf16[256,1024]{1,0:T(8,128)(2,1)}), (bf16[1024,256]{1,0:T(8,128)(2,1)}, bf16[1024,128]{1,0:T(8,128)(2,1)}, ...) | async-done | bytes 1572880 | tf_op jit(solution)/shard_map/psum | solution.py:330
  1190.1 25.2 %reduce-scatter.8.cloned.1.call-done = bf16[4,64,1024]{2,1,0:T(8,128)(2,1)} async-done(((bf16[4,256,1024]{2,1,0:T(8,128)(2,1)}), bf16[4,64,1024]{2,1,0:T(8,128)(2,1)}) %reduce-scatter.8.cloned.1.call-update) | async-done | bytes 524304 | tf_op jit(solution)/shard_map/reduce_scatter | solution.py:317
  1222.4 21.5 %all-reduce = (bf16[1024]{0:T(1024)(128)(2,1)S(1)}, bf16[1024]{0:T(1024)(128)(2,1)S(1)}) all-reduce(bf16[1024]{0:T(1024)(128)(2,1)S(1)} %get-tuple-element.217, bf16[1024]{0:T(1024)(128)(2,1)S(1)} %get-tuple-element.218), channel_id=1, replica_groups=mesh['seq'=8,'head'=4] {'seq'}, use_global_device_ids=true, to_apply=%region_21.22 | all-reduce | flops 2048 | bytes 8192 | tf_op jit(solution)/shard_map/psum | solution.py:338
  (225 shorter events, 192.2 us)
Async XLA Ops:
  7.2 480.0 %copy-start = (bf16[2,512,1024]{2,1,0:T(8,128)(2,1)S(1)}, bf16[2,512,1024]{2,1,0:T(8,128)(2,1)}, u32[]{:S(2)}) copy-start(bf16[2,512,1024]{2,1,0:T(8,128)(2,1)} %param.26) | copy-start | bytes 6291460
  7.2 30.1 %all-gather.4.cloned.1.call-start = ((), (), s32[]{:S(2)}) async-start(), calls=%async_computation.7 | async-start | bytes 2621440 | tf_op jit(solution)/shard_map/all_gather | solution.py:95
  11.8 106.0 %all-gather.6.cloned.1.call-start = ((), (), s32[]{:S(2)}) async-start(), calls=%async_computation.8 | async-start | bytes 4718592 | tf_op jit(solution)/shard_map/all_gather | solution.py:115
  12.1 34.8 %copy-start.27 = (f32[256,32]{0,1:T(8,128)}, f32[256,32]{0,1:T(8,128)S(1)}, u32[]{:S(2)}) copy-start(f32[256,32]{0,1:T(8,128)S(1)} %get-tuple-element.253) | copy-start | bytes 98308
  12.1 34.8 %copy-start.29 = (f32[256,32]{0,1:T(8,128)}, f32[256,32]{0,1:T(8,128)S(1)}, u32[]{:S(2)}) copy-start(f32[256,32]{0,1:T(8,128)S(1)} %get-tuple-element.254) | copy-start | bytes 98308
  43.0 185.8 %reduce-scatter.4.cloned.1.call-start = ((), (), s32[]{:S(2)}) async-start(), calls=%async_computation.9 | async-start | bytes 2621440 | tf_op jit(solution)/shard_map/reduce_scatter | solution.py:158
  118.9 11.9 copy-start.19
  147.8 81.1 %copy-start.5 = (bf16[4,64,1024]{2,1,0:T(8,128)(2,1)S(1)}, bf16[4,64,1024]{2,1,0:T(8,128)(2,1)}, u32[]{:S(2)}) copy-start(bf16[4,64,1024]{2,1,0:T(8,128)(2,1)} %param.17) | copy-start | bytes 1572868
  147.8 82.9 %copy-start.33 = (f32[1024]{0:T(1024)S(1)}, f32[1024]{0:T(1024)}, u32[]{:S(2)}) copy-start(f32[1024]{0:T(1024)} %param.23) | copy-start | bytes 12292
  246.1 121.1 %all-to-all-start = ((bf16[16,160,1024]{2,1,0:T(8,128)(2,1)}), bf16[16,160,1024]{2,1,0:T(8,128)(2,1)}, u32[]{:S(2)}, u32[]{:S(2)}) async-start(bf16[16,160,1024]{2,1,0:T(8,128)(2,1)} %broadcast_select_fusion), calls=%async_computation.1 | async-start | bytes 10485760 | tf_op jit(solution)/shard_map/all_to_all | solution.py:187
  367.2 120.0 %all-to-all-start.2 = ((bf16[16,160,1024]{2,1,0:T(8,128)(2,1)}), bf16[16,160,1024]{2,1,0:T(8,128)(2,1)}, u32[]{:S(2)}, u32[]{:S(2)}) async-start(bf16[16,160,1024]{2,1,0:T(8,128)(2,1)} %multiply_convert_fusion), calls=%async_computation.3 | async-start | bytes 10485760 | tf_op jit(solution)/shard_map/all_to_all | solution.py:213
  509.8 119.7 %all-to-all-start.3 = ((bf16[16,160,1024]{2,1,0:T(8,128)(2,1)}), bf16[16,160,1024]{2,1,0:T(8,128)(2,1)}, u32[]{:S(2)}, u32[]{:S(2)}) async-start(bf16[16,160,1024]{2,1,0:T(8,128)(2,1)} %bitcast.285), calls=%async_computation.4 | async-start | bytes 10485760 | tf_op jit(solution)/shard_map/all_to_all | solution.py:245
  514.6 156.6 %all-gather.8.cloned.1.call-start = ((), (), s32[]{:S(2)}) async-start(), calls=%async_computation.10 | async-start | bytes 2621440 | tf_op jit(solution)/shard_map/all_gather | solution.py:254
  650.3 315.7 %reduce-scatter.6.cloned.1.call-start = ((), (), s32[]{:S(2)}) async-start(), calls=%async_computation.11 | async-start | bytes 4718592 | tf_op jit(solution)/shard_map/reduce_scatter | solution.py:294
  650.4 28.0 %copy-start.3 = (bf16[4,256,2,2,64]{1,4,3,2,0:T(8,128)(2,1)S(1)}, bf16[4,256,2,2,64]{1,4,3,2,0:T(8,128)(2,1)}, u32[]{:S(2)}) copy-start(bf16[4,256,2,2,64]{1,4,3,2,0:T(8,128)(2,1)} %copy-done.2) | copy-start | bytes 1572868
  699.8 398.0 %all-to-all-start.1 = ((bf16[16,160,1024]{2,1,0:T(8,128)(2,1)}), bf16[16,160,1024]{2,1,0:T(8,128)(2,1)}, u32[]{:S(2)}, u32[]{:S(2)}) async-start(bf16[16,160,1024]{2,1,0:T(8,128)(2,1)} %bitcast.284), calls=%async_computation.2 | async-start | bytes 10485760 | tf_op jit(solution)/shard_map/all_to_all | solution.py:198
  798.4 289.9 %all-reduce.9.cloned.1.call-start = ((), (), s32[]{:S(2)}) async-start(), calls=%async_computation.14 | async-start | bytes 12582912 | tf_op jit(solution)/shard_map/psum | solution.py:323
  821.2 361.2 %all-reduce.7.cloned.1.call-start = ((), (), s32[]{:S(2)}) async-start(), calls=%async_computation.13 | async-start | bytes 3145728 | tf_op jit(solution)/shard_map/psum | solution.py:330
  973.2 242.0 %reduce-scatter.8.cloned.1.call-start = ((), (), s32[]{:S(2)}) async-start(), calls=%async_computation.12 | async-start | bytes 2621440 | tf_op jit(solution)/shard_map/reduce_scatter | solution.py:317
  1112.1 103.1 %copy-start.36 = (f32[1024]{0:T(1024)S(1)}, f32[1024]{0:T(1024)}, u32[]{:S(2)}) copy-start(f32[1024]{0:T(1024)} %param.18) | copy-start | bytes 12292
  1112.1 103.1 %copy-start.38 = (f32[4,64]{1,0:T(4,128)S(1)}, f32[4,64]{1,0:T(4,128)}, u32[]{:S(2)}) copy-start(f32[4,64]{1,0:T(4,128)} %copy-done.37) | copy-start | bytes 3076
  1118.0 98.7 %copy-start.43 = (bf16[1024]{0:T(1024)(128)(2,1)S(1)}, bf16[1024]{0:T(1024)(128)(2,1)}, u32[]{:S(2)}) copy-start(bf16[1024]{0:T(1024)(128)(2,1)} %get-tuple-element.171) | copy-start | bytes 6148
  1118.0 127.2 %copy-start.9 = (bf16[4,64,1024]{2,1,0:T(8,128)(2,1)S(1)}, bf16[4,64,1024]{2,1,0:T(8,128)(2,1)}, u32[]{:S(2)}) copy-start(bf16[4,64,1024]{2,1,0:T(8,128)(2,1)} %reduce-scatter.4.cloned.1.call-done) | copy-start | bytes 1572868
  1118.0 127.2 %copy-start.42 = (f32[4,64]{1,0:T(4,128)S(1)}, f32[4,64]{1,0:T(4,128)}, u32[]{:S(2)}) copy-start(f32[4,64]{1,0:T(4,128)} %get-tuple-element.249) | copy-start | bytes 3076
  (33 other events, 171.2 us)
Sparse Core Ops, SparseCore 0:
  11.9 25.2 all-gather.3
  43.2 74.6 all-gather.5
  133.0 95.7 reduce-scatter.3
  650.4 20.6 all-gather.7
  691.8 274.1 reduce-scatter.5
  969.0 119.2 all-reduce.8
  1092.7 89.6 all-reduce.6
  1184.9 30.3 reduce-scatter.7
where the time goes:
time: 1270 us; the launch traced here: 1260 us
  waiting for transfers between devices  833 us (66%)
  starting transfers between devices  115 us (9%)
  matrix products  101 us (8%)
  local copies, waits for them, and re-layouts  95 us (7%)
  other arithmetic  70 us (6%)
  blocking collectives  27.3 us (2%)
  between operations  15.3 us (1%)
    reduce_scatter x1, waiting for transfers between devices, per_device(): lax.psum_scatter(grad_kv.astype(jnp.bfloat16), 'seq', scatter_dimension=1...  137 us
    all_to_all x1, waiting for transfers between devices, per_device(): lax.all_to_all(grad_slot_in, 'seq', split_axis=0, concat_axis=0, tiled=True)  115 us
    psum x1, waiting for transfers between devices, per_device(): lax.psum(grad_gate_w.astype(jnp.bfloat16), 'head').astype(jnp.float32)  110 us
    all_to_all x1, waiting for transfers between devices, per_device(): lax.all_to_all(slot_grads, 'seq', split_axis=0, concat_axis=0, tiled=True)  99.3 us
    all_to_all x1, starting transfers between devices, per_device(): lax.all_to_all(expert_out, 'seq', split_axis=0, concat_axis=0, tiled=True)  98.7 us
    all_to_all x1, waiting for transfers between devices, per_device(): lax.all_to_all(dispatch, 'seq', split_axis=0, concat_axis=0, tiled=True)  98.4 us
    all_gather x1, waiting for transfers between devices, per_device(): kv_whole = lax.all_gather(kv_own, 'seq', axis=1, tiled=True)  70.7 us
    reduce_scatter x1, waiting for transfers between devices, per_device(): lax.psum_scatter(out_terms.astype(jnp.bfloat16), 'head', scatter_dimensio...  67.3 us
  transfers between devices with their start and end apart: 12, of which 11 were waited for; matrix products, arithmetic and copies ran while one was open for 12% of the time, Pallas kernels for 0%

commit v1 on v0

v1 whole, which is shorter than its diff:
```python
import functools
import math

import jax
import jax.numpy as jnp
from jax import lax
from jax.experimental import pallas as pl
from jax.experimental.pallas import tpu as pltpu
from jax.sharding import PartitionSpec as P

HD = 64
TOP = 8
LANES = 128

norm_eps = 1e-06
rope_base = 10000.0
masked_value = -1e30
BF = jnp.bfloat16
F32 = jnp.float32


def attn_fwd_kernel(share_ref, pay_ref, out_ref, ot_ref, lse_ref, kv_ref, kvt_ref, *, span, rows, block):
    b = pl.program_id(0)
    count = pay_ref.shape[0]

    @pl.when(b == 0)
    def _():
        def fill(i, _):
            start = pl.multiple_of(i * span, span)
            tile = pay_ref[i, pl.ds(rows, span), :]
            kv_ref[pl.ds(start, span), :] = tile
            kvt_ref[:, pl.ds(start, span)] = tile.T
            return 0
        lax.fori_loop(0, count, fill, 0)

    q_start = b * span + share_ref[0] * rows
    qt = pay_ref[b, pl.ds(0, rows), :].T * jnp.bfloat16(0.125)
    qt = jnp.concatenate([qt[:HD], qt[HD:]], 1)
    qt = jnp.concatenate([qt, jnp.zeros_like(qt)], 0)
    last = (q_start + rows - 1) // block

    def step(kb, carry, masked):
        run_max, run_sum, acc = carry
        start = pl.multiple_of(kb * block, block)
        scores = jnp.dot(kv_ref[pl.ds(start, block), :], qt, preferred_element_type=jnp.float32)
        if masked:
            keys = start + lax.broadcasted_iota(jnp.int32, scores.shape, 0)
            queries = q_start + lax.broadcasted_iota(jnp.int32, scores.shape, 1) % rows
            scores = jnp.where(keys <= queries, scores, masked_value)
        new_max = jnp.maximum(run_max, jnp.max(scores, 0, keepdims=True))
        factor = jnp.exp(run_max - new_max)
        probs = jnp.exp(scores - new_max)
        run_sum = run_sum * factor + jnp.sum(probs, 0, keepdims=True)
        acc = acc * factor + jnp.dot(
            kvt_ref[pl.ds(HD, HD), pl.ds(start, block)], probs.astype(jnp.bfloat16), preferred_element_type=jnp.float32)
        return new_max, run_sum, acc

    carry = (jnp.full((1, 2 * rows), masked_value, jnp.float32), jnp.zeros((1, 2 * rows), jnp.float32), jnp.zeros((HD, 2 * rows), jnp.float32))
    carry = lax.fori_loop(0, last, functools.partial(step, masked=False), carry)
    run_max, run_sum, acc = step(last, carry, True)
    ot = acc / run_sum
    ot_ref[0] = ot
    lse_ref[0] = jnp.broadcast_to(run_max + jnp.log(run_sum), lse_ref.shape[1:])
    out_ref[0] = jnp.concatenate([ot[:, :rows], ot[:, rows:]], 0).T.astype(jnp.bfloat16)

def attn_fwd(pay, share, span, block=512):
    n, r, _ = pay.shape
    rows = r - span
    total = n * span
    block = min(block, total)
    return pl.pallas_call(
        functools.partial(attn_fwd_kernel, span=span, rows=rows, block=block),
        out_shape=(jax.ShapeDtypeStruct((n, rows, 128), jnp.bfloat16), jax.ShapeDtypeStruct((n, HD, 2 * rows), jnp.float32), jax.ShapeDtypeStruct((n, 8, 2 * rows), jnp.float32)),
        grid_spec=pltpu.PrefetchScalarGridSpec(
            num_scalar_prefetch=1, grid=(n,),
            in_specs=[pl.BlockSpec((n, r, 128), lambda b, s: (0, 0, 0))],
            out_specs=[pl.BlockSpec((1, rows, 128), lambda b, s: (b, 0, 0)), pl.BlockSpec((1, HD, 2 * rows), lambda b, s: (b, 0, 0)), pl.BlockSpec((1, 8, 2 * rows), lambda b, s: (b, 0, 0))],
            scratch_shapes=[pltpu.VMEM((total, 128), jnp.bfloat16), pltpu.VMEM((128, total), jnp.bfloat16)],
        ),
        name="attn_fwd",
    )(share, pay)

def swap_halves(v):
    lane = lax.broadcasted_iota(jnp.int32, v.shape, v.ndim - 1)
    return jnp.where(lane % HD < HD // 2, pltpu.roll(v, 128 - HD // 2, v.ndim - 1), pltpu.roll(v, HD // 2, v.ndim - 1))

def attn_bwd_kernel(share_ref, pay_ref, go_ref, ot_ref, lse_ref, cos_ref, sin_ref, out_ref, kv_ref, kvt_ref, dk_ref, dv_ref, *, span, rows, block):
    b = pl.program_id(0)
    count = pay_ref.shape[0]

    @pl.when(b == 0)
    def _():
        def fill(i, _):
            start = pl.multiple_of(i * span, span)
            tile = pay_ref[i, pl.ds(rows, span), :]
            kv_ref[pl.ds(start, span), :] = tile
            kvt_ref[:, pl.ds(start, span)] = tile.T
            return 0
        lax.fori_loop(0, count, fill, 0)
        dk_ref[...] = jnp.zeros_like(dk_ref)
        dv_ref[...] = jnp.zeros_like(dv_ref)

    q_start = b * span + share_ref[0] * rows
    low = lax.broadcasted_iota(jnp.int32, (rows, 128), 1) < HD
    q01 = pay_ref[b, pl.ds(0, rows), :] * jnp.bfloat16(0.125)
    go01 = go_ref[0]
    zero = jnp.zeros_like(q01)
    q_rows = jnp.concatenate([jnp.where(low, q01, zero), jnp.where(low, zero, q01)], 0)
    go_rows = jnp.concatenate([jnp.where(low, go01, zero), jnp.where(low, zero, go01)], 0)
    qt = q01.T
    qt = jnp.concatenate([qt[:HD], qt[HD:]], 1)
    qt = jnp.concatenate([qt, jnp.zeros_like(qt)], 0)
    gt = go01.T
    gt = jnp.concatenate([gt[:HD], gt[HD:]], 1)
    delta = jnp.sum(gt.astype(jnp.float32) * ot_ref[0], 0, keepdims=True)
    gt = jnp.concatenate([jnp.zeros_like(gt), gt], 0)
    lse = lse_ref[0, 0:1, :]
    last = (q_start + rows - 1) // block

    def step(kb, dq, masked):
        start = pl.multiple_of(kb * block, block)
        kv = kv_ref[pl.ds(start, block), :]
        scores = jnp.dot(kv, qt, preferred_element_type=jnp.float32)
        probs = jnp.exp(scores - lse)
        if masked:
            keys = start + lax.broadcasted_iota(jnp.int32, scores.shape, 0)
            queries = q_start + lax.broadcasted_iota(jnp.int32, scores.shape, 1) % rows
            probs = jnp.where(keys <= queries, probs, 0.0)
        dprobs = jnp.dot(kv, gt, preferred_element_type=jnp.float32)
        dscores = (probs * (dprobs - delta)).astype(jnp.bfloat16)
        dv_ref[pl.ds(start, block), :] += jnp.dot(probs.astype(jnp.bfloat16), go_rows, preferred_element_type=jnp.float32)
        dk_ref[pl.ds(start, block), :] += jnp.dot(dscores, q_rows, preferred_element_type=jnp.float32)
        return dq + jnp.dot(kvt_ref[pl.ds(0, HD), pl.ds(start, block)], dscores, preferred_element_type=jnp.float32)

    dq = lax.fori_loop(0, last, functools.partial(step, masked=False), jnp.zeros((HD, 2 * rows), jnp.float32))
    dq = step(last, dq, True)
    dq = jnp.concatenate([dq[:, :rows], dq[:, rows:]], 0).T * 0.125
    at = pl.multiple_of(q_start, rows)
    dq = dq * cos_ref[pl.ds(at, rows), :] - swap_halves(dq) * sin_ref[pl.ds(at, rows), :]
    out_ref[b, pl.ds(0, rows), :] = dq.astype(jnp.bfloat16)

    @pl.when(b == count - 1)
    def _():
        def drain(i, _):
            start = pl.multiple_of(i * span, span)
            dk = dk_ref[pl.ds(start, span), :]
            dk = dk + pltpu.roll(dk, HD, 1)
            dk = dk * cos_ref[pl.ds(start, span), :] - swap_halves(dk) * sin_ref[pl.ds(start, span), :]
            dv = dv_ref[pl.ds(start, span), :]
            dv = dv + pltpu.roll(dv, HD, 1)
            lane = lax.broadcasted_iota(jnp.int32, dk.shape, 1)
            out_ref[i, pl.ds(rows, span), :] = jnp.where(lane < HD, dk, dv).astype(jnp.bfloat16)
            return 0
        lax.fori_loop(0, count, drain, 0)

def attn_bwd(pay, go, ot, lse, cos, sin, share, span, block=512):
    n, r, _ = pay.shape
    rows = r - span
    total = n * span
    block = min(block, total)
    whole = lambda *shape: pl.BlockSpec(shape, lambda b, s: (0,) * len(shape))
    return pl.pallas_call(
        functools.partial(attn_bwd_kernel, span=span, rows=rows, block=block),
        out_shape=jax.ShapeDtypeStruct((n, r, 128), jnp.bfloat16),
        grid_spec=pltpu.PrefetchScalarGridSpec(
            num_scalar_prefetch=1, grid=(n,),
            in_specs=[whole(n, r, 128), pl.BlockSpec((1, rows, 128), lambda b, s: (b, 0, 0)), pl.BlockSpec((1, HD, 2 * rows), lambda b, s: (b, 0, 0)), pl.BlockSpec((1, 8, 2 * rows), lambda b, s: (b, 0, 0)), whole(total, 128), whole(total, 128)],
            out_specs=whole(n, r, 128),
            scratch_shapes=[pltpu.VMEM((total, 128), jnp.bfloat16), pltpu.VMEM((128, total), jnp.bfloat16), pltpu.VMEM((total, 128), jnp.float32), pltpu.VMEM((total, 128), jnp.float32)],
        ),
        name="attn_bwd",
    )(share, pay, go, ot, lse, cos, sin)

def angle_tables(positions):
    half = HD // 2
    frequencies = jnp.exp(-jnp.log(rope_base) * jnp.arange(half, dtype=F32) * 2.0 / HD)
    angles = positions.astype(F32)[:, None] * frequencies[None, :]
    cosine, sine = jnp.cos(angles), jnp.sin(angles)
    return jnp.concatenate([cosine] * 4, 1), jnp.concatenate([-sine, sine] * 2, 1)


def qkv_kernel(x_ref, w_ref, cos_ref, sin_ref, out_ref, *, rows):
    span = x_ref.shape[1]
    shares = span // rows
    joint = jnp.dot(x_ref[0], w_ref[...], preferred_element_type=F32)
    low = lax.broadcasted_iota(jnp.int32, (span, LANES), 1) < HD
    cosine, sine = cos_ref[...], sin_ref[...]
    for g in range(joint.shape[1] // 256):
        query = joint[:, g * 256 : g * 256 + LANES]
        other = joint[:, g * 256 + LANES : (g + 1) * 256]
        query = (query * cosine + swap_halves(query) * sine).astype(BF)
        other = jnp.where(low, other * cosine + swap_halves(other) * sine, other).astype(BF)
        for j in range(shares):
            out_ref[g * shares + j, pl.ds(0, rows), :] = query[j * rows : (j + 1) * rows]
            out_ref[g * shares + j, pl.ds(rows, span), :] = other


def project_qkv(normed_all, w_joint, cosine, sine, rows):
    seqs, span, width = normed_all.shape
    cols = w_joint.shape[1]
    units = cols // 256 * (span // rows)
    fixed = lambda *shape: pl.BlockSpec(shape, lambda s: (0,) * len(shape))
    return pl.pallas_call(
        functools.partial(qkv_kernel, rows=rows),
        out_shape=jax.ShapeDtypeStruct((seqs * units, rows + span, LANES), BF),
        grid=(seqs,),
        in_specs=[
            pl.BlockSpec((1, span, width), lambda s: (s, 0, 0)),
            fixed(width, cols),
            fixed(span, LANES),
            fixed(span, LANES),
        ],
        out_specs=pl.BlockSpec((units, rows + span, LANES), lambda s: (s, 0, 0)),
        name="project_qkv",
    )(normed_all, w_joint, cosine, sine)


def minor_of(axis):
    return 2 if axis == "head" or lax.axis_size(axis) < 16 else 4


def place_of(axis):
    minor = minor_of(axis)
    index = lax.axis_index(axis)
    return index // minor, index % minor


def hop(value, axis, da, db):
    n, minor = lax.axis_size(axis), minor_of(axis)
    major = n // minor
    pairs = [
        (a * minor + b, (a + da) % major * minor + (b + db) % minor)
        for a in range(major)
        for b in range(minor)
    ]
    return lax.ppermute(value, axis, pairs)


def gather_slots(value, axis):
    minor = minor_of(axis)
    major = lax.axis_size(axis) // minor
    slots = []
    for a in range(major):
        if a:
            value = hop(value, axis, 1, 0)
        row, moved = [value], value
        for _ in range(1, minor):
            moved = hop(moved, axis, 0, 1)
            row.append(moved)
        slots.append(row)
    return slots


def slot_owner(axis, a, b):
    minor = minor_of(axis)
    major = lax.axis_size(axis) // minor
    my_a, my_b = place_of(axis)
    return (my_a - a) % major * minor + (my_b - b) % minor


def ring_reduce(parts, axis, da, db):
    def add(x, y):
        return (x.astype(F32) + y.astype(F32)).astype(BF)

    total = parts[1 % len(parts)]
    for part in parts[2:]:
        total = add(hop(total, axis, da, db), part)
    if len(parts) > 1:
        total = hop(total, axis, da, db).astype(F32) + parts[0].astype(F32)
    return total


def reduce_slots(slots, axis):
    rows = [ring_reduce(row, axis, 0, 1).astype(BF) for row in slots]
    return ring_reduce(rows, axis, 1, 0)


def pick(value, index):
    return lax.dynamic_index_in_dim(value, index, 0, keepdims=False)


def all_reduce(value, axis):
    minor, major = value.shape[:2]
    my_a, my_b = place_of(axis)
    total = pick(value, my_b).astype(F32)
    for d in range(1, minor):
        total = total + hop(pick(value, (my_b + d) % minor), axis, 0, d).astype(F32)
    value = total.astype(BF)
    total = pick(value, my_a).astype(F32)
    for d in range(1, major):
        total = total + hop(pick(value, (my_a + d) % major), axis, d, 0).astype(F32)
    part = total.astype(BF)
    half = lax.dynamic_update_index_in_dim(jnp.zeros(value.shape, BF), part, my_a, 0)
    for d in range(1, major):
        half = lax.dynamic_update_index_in_dim(half, hop(part, axis, d, 0), (my_a - d) % major, 0)
    whole = lax.dynamic_update_index_in_dim(jnp.zeros((minor,) + half.shape, BF), half, my_b, 0)
    for d in range(1, minor):
        whole = lax.dynamic_update_index_in_dim(whole, hop(half, axis, 0, d), (my_b - d) % minor, 0)
    return whole.astype(F32)


def small_sum(value, axis):
    minor = minor_of(axis)
    major = lax.axis_size(axis) // minor
    value = value + sum(hop(value, axis, 0, d) for d in range(1, minor))
    return value + sum(hop(value, axis, d, 0) for d in range(1, major))


def in_order(slots, axis):
    n = lax.axis_size(axis)
    whole = jnp.zeros((n,) + slots[0][0].shape, slots[0][0].dtype)
    for a, row in enumerate(slots):
        for b, block in enumerate(row):
            whole = lax.dynamic_update_index_in_dim(whole, block, slot_owner(axis, a, b), 0)
    return whole


def norm_backward(values, inv_root, gain_vec, grad_normed):
    weighted = grad_normed * gain_vec
    gain_part = jnp.sum(grad_normed * values * inv_root, (0, 1))
    grad_values = inv_root * weighted - values * (inv_root * inv_root * inv_root) * jnp.mean(
        values * weighted, -1, keepdims=True
    )
    return (grad_values, gain_part)


def dot(left, right):
    return jnp.dot(left, right, preferred_element_type=F32)


def dot_nt(left, right):
    return lax.dot_general(left, right, (((1,), (1,)), ((), ())), preferred_element_type=F32)


def dot_tn(left, right):
    return lax.dot_general(left, right, (((0,), (0,)), ((), ())), preferred_element_type=F32)


def per_device(
    hidden_in,
    norm_gain1,
    w_query,
    w_key,
    w_value,
    w_out,
    norm_gain2,
    expert_gate,
    expert_up,
    expert_down,
    routes,
    gate_weights,
    cotangent,
):
    seqs, sub, width = hidden_in.shape
    tokens = seqs * sub
    heads, ranks = lax.axis_size("head"), lax.axis_size("seq")
    kv_local = w_key.shape[1] // HD
    q_cols, k_cols = w_query.shape[1], w_key.shape[1]
    span = sub * heads
    total_len = span * ranks
    shares = ranks // (seqs * kv_local)
    rows = span // shares
    experts_local = expert_gate.shape[0]
    expert_total = experts_local * ranks
    capacity = tokens * TOP * 5 // (4 * expert_total)
    seq_rank = lax.axis_index("seq")
    head_rank = lax.axis_index("head")
    share = (seq_rank % shares).astype(jnp.int32).reshape(1)

    x_float = hidden_in.astype(F32)
    inv_one = lax.rsqrt(jnp.mean(x_float * x_float, -1, keepdims=True) + norm_eps)
    normed_one = (x_float * inv_one * norm_gain1).astype(BF)
    normed_all = in_order(gather_slots(normed_one, "head"), "head")
    normed_all = normed_all.transpose(1, 0, 2, 3).reshape(seqs, span, width)

    w_joint = jnp.concatenate(
        [
            part
            for g in range(kv_local)
            for part in (
                w_query[:, g * LANES : (g + 1) * LANES],
                w_key[:, g * HD : (g + 1) * HD],
                w_value[:, g * HD : (g + 1) * HD],
            )
        ],
        1,
    )
    cos_all, sin_all = angle_tables(jnp.arange(total_len, dtype=jnp.int32))
    cos_own = lax.dynamic_slice_in_dim(cos_all, seq_rank * span, span, 0)
    sin_own = lax.dynamic_slice_in_dim(sin_all, seq_rank * span, span, 0)

    route_tok = routes.reshape(tokens, TOP)
    gate_tok = gate_weights.reshape(tokens, TOP)
    chosen = route_tok[:, :, None] == jnp.arange(expert_total, dtype=jnp.int32)
    named = jnp.any(chosen, 1)
    gate_of = jnp.sum(jnp.where(chosen, gate_tok[:, :, None], 0.0), 1)
    order = jnp.arange(tokens, dtype=jnp.int32)
    before = (order[:, None] > order[None, :]).astype(BF)
    rank_of = dot(before, named.astype(BF))
    weight_of = jnp.where(named & (rank_of < capacity), gate_of, 0.0)
    weight_send = weight_of.reshape(tokens, ranks, experts_local).transpose(1, 2, 0)
    weight_all = lax.all_to_all(weight_send, "seq", 0, 0, tiled=True)

    pay = project_qkv(normed_all, w_joint, cos_own, sin_own, rows)
    pay = lax.all_to_all(pay, "seq", 0, 0, tiled=True)
    cot_slots = gather_slots(cotangent.reshape(tokens, width), "seq")
    w_full = in_order(gather_slots(w_out, "head"), "head").reshape(heads * q_cols, width)
    attn, attn_t, lse = attn_fwd(pay, share, span)

    def to_tokens(value):
        if shares == 1:
            value = value.reshape(ranks * heads, sub, LANES)
            value = lax.all_to_all(value, ("seq", "head"), 0, 0, tiled=True)
            value = value.reshape(seqs, kv_local, heads, sub, LANES)
            return value.transpose(0, 3, 2, 1, 4)
        value = lax.all_to_all(value, "seq", 0, 0, tiled=True)
        value = value.reshape(seqs, kv_local, heads, sub, LANES).transpose(2, 0, 1, 3, 4)
        value = lax.all_to_all(value, "head", 0, 0, tiled=True)
        return value.transpose(1, 3, 0, 2, 4)

    def to_units(value):
        if shares == 1:
            value = value.transpose(0, 3, 2, 1, 4).reshape(ranks * heads, sub, LANES)
            value = lax.all_to_all(value, ("seq", "head"), 0, 0, tiled=True)
            return value.reshape(ranks, rows, LANES)
        value = value.transpose(2, 0, 3, 1, 4)
        value = lax.all_to_all(value, "head", 0, 0, tiled=True)
        value = value.transpose(1, 2, 0, 3, 4).reshape(ranks, rows, LANES)
        return lax.all_to_all(value, "seq", 0, 0, tiled=True)

    attn_local = to_tokens(attn).reshape(tokens, heads * q_cols)
    resid = x_float + dot(attn_local, w_full).reshape(seqs, sub, width)
    inv_two = lax.rsqrt(jnp.mean(resid * resid, -1, keepdims=True) + norm_eps)
    normed_two = (resid * inv_two * norm_gain2).astype(BF).reshape(tokens, width)

    row_slots = gather_slots(normed_two, "seq")
    out_slots, grad_slots = [], []
    kept = [[] for _ in range(4)]
    for a, row in enumerate(row_slots):
        x_blk = jnp.concatenate(row, 0)
        c_blk = jnp.concatenate(cot_slots[a], 0)
        w_blk = jnp.concatenate([pick(weight_all, slot_owner("seq", a, b)) for b in range(len(row))], 1)
        out_blk, grad_blk = 0.0, 0.0
        hiddens, grads = [], []
        for e in range(experts_local):
            weight = w_blk[e][:, None]
            gate_lin = dot(x_blk, expert_gate[e])
            up_lin = dot(x_blk, expert_up[e])
            sig = jax.nn.sigmoid(gate_lin)
            silu = gate_lin * sig
            hidden = (weight * (silu * up_lin)).astype(BF)
            grad_hidden = weight * dot_nt(c_blk, expert_down[e])
            grad_up = (grad_hidden * silu).astype(BF)
            grad_gate = (grad_hidden * up_lin * sig * (1.0 + gate_lin * (1.0 - sig))).astype(BF)
            out_blk = out_blk + dot(hidden, expert_down[e])
            grad_blk = grad_blk + dot_nt(grad_gate, expert_gate[e]) + dot_nt(grad_up, expert_up[e])
            hiddens.append(hidden)
            grads.append((grad_gate, grad_up))
        kept[0].append(x_blk)
        kept[1].append(c_blk)
        kept[2].append(hiddens)
        kept[3].append(grads)
        out_blk = out_blk.astype(BF).reshape(len(row), tokens, width)
        grad_blk = grad_blk.astype(BF).reshape(len(row), tokens, width)
        out_slots.append([out_blk[b] for b in range(len(row))])
        grad_slots.append([grad_blk[b] for b in range(len(row))])

    grad_normed_two = reduce_slots(grad_slots, "seq").reshape(seqs, sub, width)
    grad_out = cotangent.astype(F32)
    grad_norm_two, gain_two_part = norm_backward(resid, inv_two, norm_gain2, grad_normed_two)
    grad_resid = grad_out + grad_norm_two
    grad_resid_b = grad_resid.astype(BF)
    grad_attn = dot_nt(grad_resid_b.reshape(tokens, width), w_full).astype(BF)
    grad_attn = to_units(grad_attn.reshape(seqs, sub, heads, kv_local, LANES))
    grad_pay = attn_bwd(pay, grad_attn, attn_t, lse, cos_all, sin_all, share, span)

    x_every, c_every = jnp.concatenate(kept[0], 0), jnp.concatenate(kept[1], 0)
    grad_gate_w, grad_up_w, grad_down_w = [], [], []
    for e in range(experts_local):
        h_every = jnp.concatenate([h[e] for h in kept[2]], 0)
        g_every = jnp.concatenate([g[e][0] for g in kept[3]], 0)
        u_every = jnp.concatenate([g[e][1] for g in kept[3]], 0)
        grad_gate_w.append(dot_tn(x_every, g_every).astype(BF))
        grad_up_w.append(dot_tn(x_every, u_every).astype(BF))
        grad_down_w.append(dot_tn(h_every, c_every).astype(BF))

    def head_total(parts):
        value = jnp.stack(parts)
        inner = value.shape[1] // (heads // 2)
        value = all_reduce(value.reshape(2, heads // 2, inner, value.shape[2]), "head")
        return value.reshape(experts_local, -1, value.shape[3])

    gate_total, up_total, down_total = head_total(grad_gate_w), head_total(grad_up_w), head_total(grad_down_w)
    mixture = reduce_slots(out_slots, "seq").reshape(seqs, sub, width)
    layer_out = (resid + mixture).astype(BF)

    def seq_total(value):
        minor = minor_of("seq")
        major = ranks // minor
        shape = value.shape
        value = value.reshape(minor, major, shape[0] // ranks, shape[1])
        return all_reduce(value, "seq").reshape(shape)

    out_w_part = dot_tn(attn_local, grad_resid_b.reshape(tokens, width)).astype(BF)
    out_w_part = out_w_part.reshape(heads, q_cols, width)
    out_w_slots = [
        [pick(out_w_part, slot_owner("head", a, b)) for b in range(2)] for a in range(heads // 2)
    ]
    out_total = seq_total(reduce_slots(out_w_slots, "head").astype(BF))

    grad_pay = lax.all_to_all(grad_pay, "seq", 0, 0, tiled=True)
    grad_q = grad_pay[:, :rows].reshape(seqs, kv_local, span, LANES)
    grad_kv = grad_pay[:, rows:].reshape(seqs, kv_local, shares, span, LANES)
    if shares == 1:
        grad_kv = grad_kv[:, :, 0]
    else:
        grad_kv = jnp.sum(grad_kv.astype(F32), 2).astype(BF)
    grad_joint = jnp.concatenate([grad_q, grad_kv], -1).transpose(0, 2, 1, 3)
    grad_joint = grad_joint.reshape(seqs * span, kv_local * 256)
    grad_w_joint = dot_tn(normed_all.reshape(seqs * span, width), grad_joint)
    joint_total = seq_total(grad_w_joint.astype(BF))
    grad_part = dot_nt(grad_joint, w_joint).astype(BF)
    grad_part = grad_part.reshape(seqs, heads, sub, width).transpose(1, 0, 2, 3)
    part_slots = [
        [pick(grad_part, slot_owner("head", a, b)) for b in range(2)] for a in range(heads // 2)
    ]
    grad_normed_one = reduce_slots(part_slots, "head")
    grad_norm_one, gain_one_part = norm_backward(x_float, inv_one, norm_gain1, grad_normed_one)
    input_grad = (grad_resid + grad_norm_one).astype(BF)
    gains = small_sum(small_sum(jnp.stack([gain_one_part, gain_two_part]), "head"), "seq")

    joint_total = joint_total.reshape(width, kv_local, 256)
    query_total = joint_total[:, :, :LANES].reshape(width, q_cols)
    key_total = joint_total[:, :, LANES : LANES + HD].reshape(width, k_cols)
    value_total = joint_total[:, :, LANES + HD :].reshape(width, k_cols)
    return (
        layer_out,
        input_grad,
        gains[0],
        query_total,
        key_total,
        value_total,
        out_total,
        gains[1],
        gate_total,
        up_total,
        down_total,
    )


def solution(mesh):
    return jax.shard_map(
        per_device,
        mesh=mesh,
        in_specs=(
            P(None, ("seq", "head"), None),
            P(),
            P(None, "head"),
            P(None, "head"),
            P(None, "head"),
            P("head", None),
            P(),
            P("seq", None, None),
            P("seq", None, None),
            P("seq", None, None),
            P(None, ("seq", "head"), None),
            P(None, ("seq", "head"), None),
            P(None, ("seq", "head"), None),
        ),
        out_specs=(
            P(None, ("seq", "head"), None),
            P(None, ("seq", "head"), None),
            P(),
            P(None, "head"),
            P(None, "head"),
            P(None, "head"),
            P("head", None),
            P(),
            P("seq", None, None),
            P("seq", None, None),
            P("seq", None, None),
        ),
        check_vma=False,
    )
```

time: 1270 us -> 585 us (0.46)
  waiting for transfers between devices: 833 us -> 165 us
  Pallas kernels: 0 us -> 45.8 us
  blocking collectives: 27.3 us -> 0 us
  matrix products: 101 us -> 76.8 us
  other arithmetic: 70 us -> 49.6 us
  local copies, waits for them, and re-layouts: 95 us -> 113 us
    all_to_all x4 -> x5, waiting for transfers between devices: 312 us -> 0.92 us  [the longest x1 0.91 us: to_tokens(): value = lax.all_to_all(value, ('seq', 'head'), 0, 0, tiled=True)]
    reduce_scatter x3 -> x0, waiting for transfers between devices: 229 us -> none  [the longest x1 137 us: per_device(): lax.psum_scatter(grad_kv.astype(jnp.bfloat16), 'seq', scatter_dimension=1...]
    psum x2 -> x0, waiting for transfers between devices: 175 us -> none  [the longest x1 110 us: per_device(): lax.psum(grad_gate_w.astype(jnp.bfloat16), 'head').astype(jnp.float32)]
    ppermute x0 -> x74, waiting for transfers between devices: none -> 164 us  [hop(): return lax.ppermute(value, axis, pairs)]
    all_gather x3 -> x0, waiting for transfers between devices: 117 us -> none  [the longest x1 70.7 us: per_device(): kv_whole = lax.all_gather(kv_own, 'seq', axis=1, tiled=True)]
    ppermute x0 -> x74, starting transfers between devices: none -> 87.4 us  [hop(): return lax.ppermute(value, axis, pairs)]
    all_to_all x4 -> x5, starting transfers between devices: 114 us -> 32.5 us  [the longest x1 9.8 us: to_tokens(): value = lax.all_to_all(value, ('seq', 'head'), 0, 0, tiled=True)]
    gather x5 -> x0, local copies, waits for them, and re-layouts: 59.9 us -> none  [the longest x1 14.4 us: per_device(): returned_flat[slot_safe].astype(jnp.float32) * pair_weight[:, None]]
  transfers between devices with their start and end apart: 12 -> 79, of which waited for: 11 -> 28; matrix products, arithmetic and copies ran while one was open for 12% -> 39% of each run, Pallas kernels for 0% -> 8%
where the time goes in v1:
time: 585 us; the launch traced here: 573 us
  waiting for transfers between devices  165 us (28%)
  starting transfers between devices  120 us (21%)
  local copies, waits for them, and re-layouts  113 us (19%)
  matrix products  76.8 us (13%)
  other arithmetic  49.6 us (8%)
  Pallas kernels  45.8 us (8%)
    ppermute x74, waiting for transfers between devices, hop(): return lax.ppermute(value, axis, pairs)  164 us
    ppermute x74, starting transfers between devices, hop(): return lax.ppermute(value, axis, pairs)  87.4 us
    dot_general x26, matrix products, dot_nt(): lax.dot_general(left, right, (((1,), (1,)), ((), ())), preferred_element_...  30.1 us
    dynamic_update_slice x9, local copies, waits for them, and re-layouts, all_reduce(): lax.dynamic_update_index_in_dim(half, hop(part, axis, d, 0), (my_a - d) %...  26.2 us
    dot_general x26, matrix products, dot(): return jnp.dot(left, right, preferred_element_type=F32)  24.7 us
    unnamed x146, local copies, waits for them, and re-layouts  24.2 us
    pallas_call x1, Pallas kernels, attn_bwd(): pl.pallas_call(functools.partial(attn_bwd_kernel, span=span, rows=rows, b...  23.8 us
    dot_general x8, matrix products, dot_tn(): lax.dot_general(left, right, (((0,), (0,)), ((), ())), preferred_element_...  22 us
  transfers between devices with their start and end apart: 79, of which 28 were waited for; matrix products, arithmetic and copies ran while one was open for 39% of the time, Pallas kernels for 8%

profile of v1, /device:TPU:0, one launch (start us, length us, event | category | flops | bytes accessed | tf_op | source)
XLA Modules:
  0.0 573.2 jit_solution(14372712286387334154)
XLA Ops:
  7.9 5.8 %all-to-all-start.2 = ((f32[8,2,256]{2,1,0:T(2,128)}), f32[8,2,256]{2,1,0:T(2,128)S(1)}, u32[]{:S(2)}, u32[]{:S(2)}) async-start(f32[8,2,256]{2,1,0:T(2,128)} %bitcast.19), calls=%async_computation.2 | async-start | bytes 32768 | tf_op jit(solution)/shard_map/all_to_all | solution.py:402
  34.1 5.5 project_qkv.1
  39.6 6.1 %all-to-all-start = ((bf16[8,512,128]{2,1,0:T(8,128)(2,1)}), bf16[8,512,128]{2,1,0:T(8,128)(2,1)S(1)}, u32[]{:S(2)}, u32[]{:S(2)}) async-start(bf16[8,512,128]{2,1,0:T(8,128)(2,1)} %project_qkv.1), calls=%async_computation | async-start | bytes 2097152 | tf_op jit(solution)/shard_map/all_to_all | solution.py:405
  54.0 24.8 %collective-permute-done.20 = bf16[256,1024]{1,0:T(8,128)(2,1)S(1)} collective-permute-done((bf16[256,1024]{1,0:T(8,128)(2,1)S(1)}, bf16[256,1024]{1,0:T(8,128)(2,1)S(1)}, u32[]{:S(2)}, u32[]{:S(2)}) %collective-permute-start.20) | collective-permute-done | bytes 524320 | tf_op jit(solution)/shard_map/ppermute | solution.py:236
  87.6 16.5 %attn_fwd.1 = (bf16[8,256,128]{2,1,0:T(8,128)(2,1)}, f32[8,64,512]{2,1,0:T(8,128)}, f32[8,8,512]{2,1,0:T(8,128)}) custom-call(s32[1]{0:T(128)} %constant.565.clone.1.share_ref, bf16[8,512,128]{2,1,0:T(8,128)(2,1)} %copy-done.5), custom_call_target="tpu_custom_call" | custom-call | tf_op jit(solution)/shard_map/attn_fwd/pallas_call | solution.py:71
  104.1 9.8 %all-to-all-start.1 = ((bf16[32,64,128]{2,1,0:T(8,128)(2,1)}), bf16[32,64,128]{2,1,0:T(8,128)(2,1)S(1)}, u32[]{:S(2)}, u32[]{:S(2)}) async-start(bf16[32,64,128]{2,1,0:T(8,128)(2,1)} %bitcast.481), calls=%async_computation.1 | async-start | bytes 1048576 | tf_op jit(solution)/shard_map/all_to_all | solution.py:413
  126.5 11.8 %collective-permute-done.28 = bf16[256,1024]{1,0:T(8,128)(2,1)} collective-permute-done((bf16[256,1024]{1,0:T(8,128)(2,1)}, bf16[256,1024]{1,0:T(8,128)(2,1)}, u32[]{:S(2)}, u32[]{:S(2)}) %collective-permute-start.28) | collective-permute-done | bytes 524320 | tf_op jit(solution)/shard_map/ppermute | solution.py:236
  184.6 11.5 %collective-permute-start.10 = (bf16[256,1024]{1,0:T(8,128)(2,1)}, bf16[256,1024]{1,0:T(8,128)(2,1)S(1)}, u32[]{:S(2)}, u32[]{:S(2)}) collective-permute-start(bf16[256,1024]{1,0:T(8,128)(2,1)} %collective-permute-done.6), channel_id=1, source_target_pairs={{0,8},{4,12},{8,16},{12,20},{16,24},{20,28},{24,0},{28,4},{1,9},{5... | collective-permute-start | bytes 1572872 | tf_op jit(solution)/shard_map/ppermute | solution.py:236
  198.4 6.3 %collective-permute-done.7 = bf16[256,1024]{1,0:T(8,128)(2,1)S(1)} collective-permute-done((bf16[256,1024]{1,0:T(8,128)(2,1)}, bf16[256,1024]{1,0:T(8,128)(2,1)S(1)}, u32[]{:S(2)}, u32[]{:S(2)}) %collective-permute-start.7) | collective-permute-done | bytes 524320 | tf_op jit(solution)/shard_map/ppermute | solution.py:236
  218.8 20.8 %collective-permute-done.11 = bf16[256,1024]{1,0:T(8,128)(2,1)S(1)} collective-permute-done((bf16[256,1024]{1,0:T(8,128)(2,1)S(1)}, bf16[256,1024]{1,0:T(8,128)(2,1)S(1)}, u32[]{:S(2)}, u32[]{:S(2)}) %collective-permute-start.11) | collective-permute-done | bytes 524320 | tf_op jit(solution)/shard_map/ppermute | solution.py:236
  257.1 7.7 %collective-permute-done.15 = bf16[256,1024]{1,0:T(8,128)(2,1)S(1)} collective-permute-done((bf16[256,1024]{1,0:T(8,128)(2,1)S(1)}, bf16[256,1024]{1,0:T(8,128)(2,1)S(1)}, u32[]{:S(2)}, u32[]{:S(2)}) %collective-permute-start.15) | collective-permute-done | bytes 524320 | tf_op jit(solution)/shard_map/ppermute | solution.py:236
  351.7 6.2 %collective-permute-done.63 = bf16[512,512]{1,0:T(8,128)(2,1)S(1)} collective-permute-done((bf16[512,512]{1,0:T(8,128)(2,1)S(1)}, bf16[512,512]{1,0:T(8,128)(2,1)S(1)}, u32[]{:S(2)}, u32[]{:S(2)}) %collective-permute-start.63) | collective-permute-done | bytes 524320 | tf_op jit(solution)/shard_map/ppermute | solution.py:236
  360.4 8.8 %collective-permute-done.67 = bf16[512,512]{1,0:T(8,128)(2,1)S(1)} collective-permute-done((bf16[512,512]{1,0:T(8,128)(2,1)S(1)}, bf16[512,512]{1,0:T(8,128)(2,1)S(1)}, u32[]{:S(2)}, u32[]{:S(2)}) %collective-permute-start.67) | collective-permute-done | bytes 524320 | tf_op jit(solution)/shard_map/ppermute | solution.py:236
  371.6 8.8 %collective-permute-done.71 = bf16[256,1024]{1,0:T(8,128)(2,1)S(1)} collective-permute-done((bf16[256,1024]{1,0:T(8,128)(2,1)S(1)}, bf16[256,1024]{1,0:T(8,128)(2,1)S(1)}, u32[]{:S(2)}, u32[]{:S(2)}) %collective-permute-start.71) | collective-permute-done | bytes 524320 | tf_op jit(solution)/shard_map/ppermute | solution.py:236
  384.2 23.8 %attn_bwd.1 = bf16[8,512,128]{2,1,0:T(8,128)(2,1)} custom-call(s32[1]{0:T(128)} %constant.565.clone.1.share_ref, bf16[8,512,128]{2,1,0:T(8,128)(2,1)} %copy-done.5, bf16[8,256,128]{2,1,0:T(8,128)(2,1)} %bitcast.49.go_ref, f32[8,64,512]{2,1,0:T(8,128)} %get-tuple-element.15.ot_ref, f32[8,8,512]{2,1,0:T(8,128)} %get-tuple-element.16.lse_ref, ...), custom_call_target="tpu_custom_call" | custom-call | tf_op jit(solution)/shard_map/attn_bwd/pallas_call | solution.py:162
  420.4 9.8 %collective-permute-done.54 = bf16[4,32,1024]{2,1,0:T(8,128)(2,1)S(1)} collective-permute-done((bf16[4,32,1024]{2,1,0:T(8,128)(2,1)S(1)}, bf16[4,32,1024]{2,1,0:T(8,128)(2,1)S(1)}, u32[]{:S(2)}, u32[]{:S(2)}) %collective-permute-start.54) | collective-permute-done | bytes 262176 | tf_op jit(solution)/shard_map/ppermute | solution.py:236
  438.3 5.6 collective-permute-done.56
  480.2 6.9 %collective-permute-done.43 = bf16[4,128,512]{2,1,0:T(8,128)(2,1)S(1)} collective-permute-done((bf16[4,128,512]{2,1,0:T(8,128)(2,1)S(1)}, bf16[4,128,512]{2,1,0:T(8,128)(2,1)S(1)}, u32[]{:S(2)}, u32[]{:S(2)}) %collective-permute-start.43) | collective-permute-done | bytes 524320 | tf_op jit(solution)/shard_map/ppermute | solution.py:236
  494.0 6.5 %collective-permute-done.45 = bf16[128,512]{1,0:T(8,128)(2,1)S(1)} collective-permute-done((bf16[128,512]{1,0:T(8,128)(2,1)S(1)}, bf16[128,512]{1,0:T(8,128)(2,1)S(1)}, u32[]{:S(2)}, u32[]{:S(2)}) %collective-permute-start.45) | collective-permute-done | bytes 131104 | tf_op jit(solution)/shard_map/ppermute | solution.py:236
  511.0 5.6 dynamic_update_slice.114
  521.6 7.4 %dynamic_update_slice.115 = bf16[4,128,512]{1,0,2:T(4,128)(2,1)} dynamic-update-slice(bf16[4,128,512]{1,0,2:T(4,128)(2,1)} %copy-done.33, bf16[1,128,512]{1,0,2:T(2,128)(2,1)S(1)} %copy.86, s32[]{:T(128)S(6)} %select_n.485, s32[]{:T(128)} %constant.572.clone.1, s32[]{:T(128)} %constant.572.clone.1) | dynamic-update-slice | bytes 262148 | tf_op jit(solution)/shard_map/jit(dynamic_update_index_in_dim)/dynamic_update_slice | solution.py:295
  528.9 7.4 %dynamic_update_slice.116 = bf16[4,128,512]{1,0,2:T(4,128)(2,1)} dynamic-update-slice(bf16[4,128,512]{1,0,2:T(4,128)(2,1)} %dynamic_update_slice.115, bf16[1,128,512]{1,0,2:T(2,128)(2,1)} %copy.87, s32[]{:T(128)S(6)} %select_n.486, s32[]{:T(128)} %constant.572.clone.1, s32[]{:T(128)} %constant.572.clone.1) | dynamic-update-slice | bytes 262148 | tf_op jit(solution)/shard_map/jit(dynamic_update_index_in_dim)/dynamic_update_slice | solution.py:295
  536.3 7.4 %dynamic_update_slice.117 = bf16[4,128,512]{1,0,2:T(4,128)(2,1)} dynamic-update-slice(bf16[4,128,512]{1,0,2:T(4,128)(2,1)} %dynamic_update_slice.116, bf16[1,128,512]{1,0,2:T(2,128)(2,1)} %copy.88, s32[]{:T(128)S(6)} %select_n.487, s32[]{:T(128)} %constant.572.clone.1, s32[]{:T(128)} %constant.572.clone.1) | dynamic-update-slice | bytes 262148 | tf_op jit(solution)/shard_map/jit(dynamic_update_index_in_dim)/dynamic_update_slice | solution.py:295
  551.0 7.5 %collective-permute-done.39 = f32[2,1024]{1,0:T(2,128)S(1)} collective-permute-done((f32[2,1024]{1,0:T(2,128)S(1)}, f32[2,1024]{1,0:T(2,128)S(1)}, u32[]{:S(2)}, u32[]{:S(2)}) %collective-permute-start.39) | collective-permute-done | bytes 8224 | tf_op jit(solution)/shard_map/ppermute | solution.py:236
  (479 shorter events, 331.9 us)
Async XLA Ops:
  7.9 31.6 %all-to-all-start.2 = ((f32[8,2,256]{2,1,0:T(2,128)}), f32[8,2,256]{2,1,0:T(2,128)S(1)}, u32[]{:S(2)}, u32[]{:S(2)}) async-start(f32[8,2,256]{2,1,0:T(2,128)} %bitcast.19), calls=%async_computation.2 | async-start | bytes 32768 | tf_op jit(solution)/shard_map/all_to_all | solution.py:402
  39.6 47.0 %all-to-all-start = ((bf16[8,512,128]{2,1,0:T(8,128)(2,1)}), bf16[8,512,128]{2,1,0:T(8,128)(2,1)S(1)}, u32[]{:S(2)}, u32[]{:S(2)}) async-start(bf16[8,512,128]{2,1,0:T(8,128)(2,1)} %project_qkv.1), calls=%async_computation | async-start | bytes 2097152 | tf_op jit(solution)/shard_map/all_to_all | solution.py:405
  45.7 68.2 %collective-permute-start.3 = (bf16[256,1024]{1,0:T(8,128)(2,1)}, bf16[256,1024]{1,0:T(8,128)(2,1)}, u32[]{:S(2)}, u32[]{:S(2)}) collective-permute-start(bf16[256,1024]{1,0:T(8,128)(2,1)} %param.18), channel_id=1, source_target_pairs={{0,1},{1,0},{2,3},{3,2},{4,5},{5,4},{6,7},{7,6},{8,9},{9,8},{10,11... | collective-permute-start | bytes 1572872 | tf_op jit(solution)/shard_map/ppermute | solution.py:236
  45.9 37.7 %collective-permute-start.4 = (bf16[256,1024]{1,0:T(8,128)(2,1)}, bf16[256,1024]{1,0:T(8,128)(2,1)}, u32[]{:S(2)}, u32[]{:S(2)}) collective-permute-start(bf16[256,1024]{1,0:T(8,128)(2,1)} %param.18), channel_id=1, source_target_pairs={{0,2},{1,3},{2,0},{3,1},{4,6},{5,7},{6,4},{7,5},{8,10},{9,11},{10,... | collective-permute-start | bytes 1572872 | tf_op jit(solution)/shard_map/ppermute | solution.py:236
  46.4 37.2 %collective-permute-start.32 = (bf16[256,1024]{1,0:T(8,128)(2,1)S(1)}, bf16[256,1024]{1,0:T(8,128)(2,1)}, u32[]{:S(2)}, u32[]{:S(2)}) collective-permute-start(bf16[256,1024]{1,0:T(8,128)(2,1)S(1)} %bitcast.443), channel_id=1, source_target_pairs={{0,4},{4,0},{8,12},{12,8},{16,20},{20,16},{24,28},{28,24},{1,5},{5... | collective-permute-start | bytes 1572872 | tf_op jit(solution)/shard_map/ppermute | solution.py:236
  78.9 42.4 %collective-permute-start.21 = (bf16[256,1024]{1,0:T(8,128)(2,1)S(1)}, bf16[256,1024]{1,0:T(8,128)(2,1)S(1)}, u32[]{:S(2)}, u32[]{:S(2)}) collective-permute-start(bf16[256,1024]{1,0:T(8,128)(2,1)S(1)} %collective-permute-done.20), channel_id=1, source_target_pairs={{0,4},{4,0},{8,12},{12,8},{16,20},{20,16},{24,28},{28,24},{1,5},{5... | collective-permute-start | bytes 1572872 | tf_op jit(solution)/shard_map/ppermute | solution.py:236
  80.3 37.4 %collective-permute-start.24 = (bf16[256,1024]{1,0:T(8,128)(2,1)S(1)}, bf16[256,1024]{1,0:T(8,128)(2,1)}, u32[]{:S(2)}, u32[]{:S(2)}) collective-permute-start(bf16[256,1024]{1,0:T(8,128)(2,1)S(1)} %collective-permute-done.20), channel_id=1, source_target_pairs={{0,8},{4,12},{8,16},{12,20},{16,24},{20,28},{24,0},{28,4},{1,9},{5... | collective-permute-start | bytes 1572872 | tf_op jit(solution)/shard_map/ppermute | solution.py:236
  83.6 41.0 %collective-permute-start.5 = (bf16[256,1024]{1,0:T(8,128)(2,1)}, bf16[256,1024]{1,0:T(8,128)(2,1)}, u32[]{:S(2)}, u32[]{:S(2)}) collective-permute-start(bf16[256,1024]{1,0:T(8,128)(2,1)} %collective-permute-done.4), channel_id=1, source_target_pairs={{0,1},{1,0},{2,3},{3,2},{4,5},{5,4},{6,7},{7,6},{8,9},{9,8},{10,11... | collective-permute-start | bytes 1572872 | tf_op jit(solution)/shard_map/ppermute | solution.py:236
  104.1 36.7 %all-to-all-start.1 = ((bf16[32,64,128]{2,1,0:T(8,128)(2,1)}), bf16[32,64,128]{2,1,0:T(8,128)(2,1)S(1)}, u32[]{:S(2)}, u32[]{:S(2)}) async-start(bf16[32,64,128]{2,1,0:T(8,128)(2,1)} %bitcast.481), calls=%async_computation.1 | async-start | bytes 1048576 | tf_op jit(solution)/shard_map/all_to_all | solution.py:413
  178.6 138.6 %collective-permute-start.33 = (bf16[256,1024]{1,0:T(8,128)(2,1)S(1)}, bf16[256,1024]{1,0:T(8,128)(2,1)S(1)}, u32[]{:S(2)}, u32[]{:S(2)}) collective-permute-start(bf16[256,1024]{1,0:T(8,128)(2,1)S(1)} %slice.252), channel_id=1, source_target_pairs={{0,4},{4,0},{8,12},{12,8},{16,20},{20,16},{24,28},{28,24},{1,5},{5... | collective-permute-start | bytes 1572872 | tf_op jit(solution)/shard_map/ppermute | solution.py:236
  183.1 162.9 %collective-permute-start.19 = (bf16[256,1024]{1,0:T(8,128)(2,1)}, bf16[256,1024]{1,0:T(8,128)(2,1)}, u32[]{:S(2)}, u32[]{:S(2)}) collective-permute-start(bf16[256,1024]{1,0:T(8,128)(2,1)} %slice.244), channel_id=1, source_target_pairs={{0,4},{4,0},{8,12},{12,8},{16,20},{20,16},{24,28},{28,24},{1,5},{5... | collective-permute-start | bytes 1572872 | tf_op jit(solution)/shard_map/ppermute | solution.py:236
  217.2 39.1 %collective-permute-start.8 = (bf16[256,1024]{1,0:T(8,128)(2,1)S(1)}, bf16[256,1024]{1,0:T(8,128)(2,1)S(1)}, u32[]{:S(2)}, u32[]{:S(2)}) collective-permute-start(bf16[256,1024]{1,0:T(8,128)(2,1)S(1)} %slice.232), channel_id=1, source_target_pairs={{0,4},{4,0},{8,12},{12,8},{16,20},{20,16},{24,28},{28,24},{1,5},{5... | collective-permute-start | bytes 1572872 | tf_op jit(solution)/shard_map/ppermute | solution.py:236
  243.6 39.2 %collective-permute-start.23 = (bf16[256,1024]{1,0:T(8,128)(2,1)S(1)}, bf16[256,1024]{1,0:T(8,128)(2,1)S(1)}, u32[]{:S(2)}, u32[]{:S(2)}) collective-permute-start(bf16[256,1024]{1,0:T(8,128)(2,1)S(1)} %add_convert_fusion.14), channel_id=1, source_target_pairs={{0,8},{4,12},{8,16},{12,20},{16,24},{20,28},{24,0},{28,4},{1,9},{5... | collective-permute-start | bytes 1572872 | tf_op jit(solution)/shard_map/ppermute | solution.py:236
  329.0 55.1 %all-to-all-start.3 = ((bf16[32,64,128]{2,1,0:T(8,128)(2,1)}), bf16[32,64,128]{2,1,0:T(8,128)(2,1)}, u32[]{:S(2)}, u32[]{:S(2)}) async-start(bf16[32,64,128]{2,1,0:T(8,128)(2,1)} %bitcast.465), calls=%async_computation.3 | async-start | bytes 1048576 | tf_op jit(solution)/shard_map/all_to_all | solution.py:424
  339.7 73.6 %collective-permute-start.53 = (bf16[256,1024]{1,0:T(8,128)(2,1)}, bf16[256,1024]{1,0:T(8,128)(2,1)}, u32[]{:S(2)}, u32[]{:S(2)}) collective-permute-start(bf16[256,1024]{1,0:T(8,128)(2,1)} %get-tuple-element.65), channel_id=1, source_target_pairs={{0,1},{1,0},{2,3},{3,2},{4,5},{5,4},{6,7},{7,6},{8,9},{9,8},{10,11... | collective-permute-start | bytes 1572872 | tf_op jit(solution)/shard_map/ppermute | solution.py:236
  346.3 34.2 %collective-permute-start.71 = (bf16[256,1024]{1,0:T(8,128)(2,1)S(1)}, bf16[256,1024]{1,0:T(8,128)(2,1)S(1)}, u32[]{:S(2)}, u32[]{:S(2)}) collective-permute-start(bf16[256,1024]{1,0:T(8,128)(2,1)S(1)} %dynamic-slice_bitcast_fusion), channel_id=1, source_target_pairs={{0,2},{1,3},{2,0},{3,1},{4,6},{5,7},{6,4},{7,5},{8,10},{9,11},{10,... | collective-permute-start | bytes 1572872 | tf_op jit(solution)/shard_map/ppermute | solution.py:236
  351.5 61.8 %collective-permute-start.52 = (bf16[256,1024]{1,0:T(8,128)(2,1)}, bf16[256,1024]{1,0:T(8,128)(2,1)}, u32[]{:S(2)}, u32[]{:S(2)}) collective-permute-start(bf16[256,1024]{1,0:T(8,128)(2,1)} %fusion.97), channel_id=1, source_target_pairs={{0,2},{1,3},{2,0},{3,1},{4,6},{5,7},{6,4},{7,5},{8,10},{9,11},{10,... | collective-permute-start | bytes 1572872 | tf_op jit(solution)/shard_map/ppermute | solution.py:236
  359.0 58.1 %collective-permute-start.64 = (bf16[512,512]{1,0:T(8,128)(2,1)}, bf16[512,512]{1,0:T(8,128)(2,1)}, u32[]{:S(2)}, u32[]{:S(2)}) collective-permute-start(bf16[512,512]{1,0:T(8,128)(2,1)} %get-tuple-element.59), channel_id=1, source_target_pairs={{0,2},{1,3},{2,0},{3,1},{4,6},{5,7},{6,4},{7,5},{8,10},{9,11},{10,... | collective-permute-start | bytes 1572872 | tf_op jit(solution)/shard_map/ppermute | solution.py:236
  370.2 48.3 %collective-permute-start.68 = (bf16[512,512]{1,0:T(8,128)(2,1)}, bf16[512,512]{1,0:T(8,128)(2,1)}, u32[]{:S(2)}, u32[]{:S(2)}) collective-permute-start(bf16[512,512]{1,0:T(8,128)(2,1)} %get-tuple-element.57), channel_id=1, source_target_pairs={{0,2},{1,3},{2,0},{3,1},{4,6},{5,7},{6,4},{7,5},{8,10},{9,11},{10,... | collective-permute-start | bytes 1572872 | tf_op jit(solution)/shard_map/ppermute | solution.py:236
  382.8 61.2 %collective-permute-start.72 = (bf16[256,1024]{1,0:T(8,128)(2,1)}, bf16[256,1024]{1,0:T(8,128)(2,1)}, u32[]{:S(2)}, u32[]{:S(2)}) collective-permute-start(bf16[256,1024]{1,0:T(8,128)(2,1)} %get-tuple-element.55), channel_id=1, source_target_pairs={{0,2},{1,3},{2,0},{3,1},{4,6},{5,7},{6,4},{7,5},{8,10},{9,11},{10,... | collective-permute-start | bytes 1572872 | tf_op jit(solution)/shard_map/ppermute | solution.py:236
  407.9 58.2 %all-to-all-start.4 = ((bf16[8,512,128]{2,1,0:T(8,128)(2,1)}), bf16[8,512,128]{2,1,0:T(8,128)(2,1)}, u32[]{:S(2)}, u32[]{:S(2)}) async-start(bf16[8,512,128]{2,1,0:T(8,128)(2,1)} %attn_bwd.1), calls=%async_computation.4 | async-start | bytes 2097152 | tf_op jit(solution)/shard_map/all_to_all | solution.py:511
  418.1 44.1 %collective-permute-start.65 = (bf16[2,512,512]{2,1,0:T(8,128)(2,1)S(1)}, bf16[2,512,512]{2,1,0:T(8,128)(2,1)S(1)}, u32[]{:S(2)}, u32[]{:S(2)}) collective-permute-start(bf16[2,512,512]{2,1,0:T(8,128)(2,1)S(1)} %bitcast_dynamic-update-slice_fusion.15), channel_id=1, source_target_pairs={{0,1},{1,0},{2,3},{3,2},{4,5},{5,4},{6,7},{7,6},{8,9},{9,8},{10,11... | collective-permute-start | bytes 3145736 | tf_op jit(solution)/shard_map/ppermute | solution.py:236
  445.9 44.5 %collective-permute-start.73 = (bf16[2,256,1024]{2,1,0:T(8,128)(2,1)}, bf16[2,256,1024]{2,1,0:T(8,128)(2,1)}, u32[]{:S(2)}, u32[]{:S(2)}) collective-permute-start(bf16[2,256,1024]{2,1,0:T(8,128)(2,1)} %bitcast_dynamic-update-slice_fusion.11), channel_id=1, source_target_pairs={{0,1},{1,0},{2,3},{3,2},{4,5},{5,4},{6,7},{7,6},{8,9},{9,8},{10,11... | collective-permute-start | bytes 3145736 | tf_op jit(solution)/shard_map/ppermute | solution.py:236
  508.1 36.9 %collective-permute-start.37 = (f32[2,1024]{1,0:T(2,128)}, f32[2,1024]{1,0:T(2,128)}, u32[]{:S(2)}, u32[]{:S(2)}) collective-permute-start(f32[2,1024]{1,0:T(2,128)} %pad_maximum_fusion.7), channel_id=1, source_target_pairs={{0,1},{1,0},{2,3},{3,2},{4,5},{5,4},{6,7},{7,6},{8,9},{9,8},{10,11... | collective-permute-start | bytes 24584 | tf_op jit(solution)/shard_map/ppermute | solution.py:236
  (118 other events, 1788.4 us)
